TPU v7x, 32 devices: a whole 2x2x4 slice. The times are simulated.
32 devices in a mesh: groups: 2 (over y), fsdp: 4 (over z), mp: 2 (over x), sub: 2 (over core).
Axes of the slice: x: 2, y: 2, z: 4, core: 2. Of those that a mesh axis runs over, the one named last changes fastest.
Arguments:
- hidden: bfloat16 [128, 36864], P(('groups', 'fsdp', 'sub'), 'mp'), parts along dimension 0, may hold values from -6 to 6
- residual: bfloat16 [128, 4608], P(('groups', 'fsdp', 'sub')), parts along dimension 0, may hold values from -6 to 6
- down_packed: int32 [4608, 4608], P('mp', 'fsdp'), may hold values from -2147483648 to 2147483646
- down_scale: bfloat16 [288, 4608], P('mp', 'fsdp'), may hold values from 0.00049972534 to 0.0019989014
- post_gain: float32 [4608], replicated, may hold values from 0.1 to 1.9
- final_gain: float32 [4608], replicated, may hold values from 0.1 to 1.9
- embed_packed: int32 [8192, 576], P(('fsdp', 'mp', 'sub')), may hold values from -2147483648 to 2147483646
- embed_scale: bfloat16 [8192, 36], P(('fsdp', 'mp', 'sub')), may hold values from 0.0059814453 to 0.029907227
- targets: int32 [128], P(('groups', 'fsdp', 'sub')), parts along dimension 0, may hold values from 0 to 8191
- loss_mask: int32 [128], P(('groups', 'fsdp', 'sub')), parts along dimension 0, may hold values 0 or 1
Outputs:
- token_loss: float32 [128], P(('groups', 'fsdp', 'sub')), parts along dimension 0
- mean_loss: float32 [2], P('groups'), parts along dimension 0
There are 2 independent parts, one for each index of `groups`. A program takes and returns all parts, laid end to end along the dimension named above; an argument that names none is the same for every part. Nothing has to cross between parts.
Inputs may be any that keep to these rules, and one draw needn't show every extreme that they name: `down_packed`: bits 4 k to 4 k + 3 of the word in row r hold the signed code of row 8 r + k of the down projection, k = 0..7. `embed_packed`: bits 4 k to 4 k + 3 of the word in column j hold the signed code of column k * 576 + j of the embedding, k = 0..7.
All inputs are finite; a program needn't handle non-finite values. No bound on the sum of `loss_mask` on one device may be relied on, other than what follows from the above.
Results may differ from a plain program's by a relative error of at most 0.00097.
Values may be sent and summed in bfloat16 or wider, within the bound.
A program may use at most 128 MiB of HBM per device.

v0:
```python
import jax
import jax.numpy as jnp
from jax import lax
from jax.sharding import PartitionSpec as P

EPS = 1e-06
CAP = 30.0


def signed_planes(words):
    shifts = (28 - 4 * jnp.arange(8, dtype=jnp.int32))[None, :, None]
    lifted = jnp.left_shift(words[:, None, :], shifts)
    return jnp.right_shift(lifted, 28)


def dequant_down(words, scales):
    cols = words.shape[1]
    codes = signed_planes(words).astype(jnp.bfloat16)
    grouped = codes.reshape(scales.shape[0], -1, cols) * scales[:, None, :]
    return grouped.reshape(-1, cols)


def dequant_embed(words, scales):
    rows = words.shape[0]
    codes = signed_planes(words).astype(jnp.bfloat16)
    grouped = codes.reshape(rows, scales.shape[1], -1) * scales[:, :, None]
    return grouped.reshape(rows, -1)


def normalize_rows(ffn, residual, post_gain, final_gain):
    ffn = lax.psum(ffn, "mp")
    normed = ffn * lax.rsqrt(jnp.mean(ffn * ffn, axis=-1, keepdims=True) + EPS) * post_gain
    stream = residual.astype(jnp.float32) + normed
    return (
        stream * lax.rsqrt(jnp.mean(stream * stream, axis=-1, keepdims=True) + EPS) * final_gain
    ).astype(jnp.bfloat16)


def on_device(
    hidden,
    residual,
    down_packed,
    down_scale,
    post_gain,
    final_gain,
    embed_packed,
    embed_scale,
    targets,
    loss_mask,
):
    tok_rows = hidden.shape[0]
    local_weight = dequant_down(down_packed, down_scale)
    partial_cols = jnp.dot(
        lax.all_gather(hidden, "fsdp", axis=0, tiled=True),
        local_weight,
        preferred_element_type=jnp.float32,
    )
    ffn = lax.all_to_all(partial_cols, "fsdp", split_axis=0, concat_axis=1, tiled=True)
    states = normalize_rows(ffn, residual, post_gain, final_gain)
    all_states, all_targets = (
        lax.all_gather(states, ("fsdp", "sub"), axis=0, tiled=True),
        lax.all_gather(targets, ("fsdp", "sub"), axis=0, tiled=True),
    )
    embed = dequant_embed(embed_packed, embed_scale)
    logits = lax.dot_general(
        all_states, embed, (((1,), (1,)), ((), ())), preferred_element_type=jnp.float32
    )
    capped = CAP * jnp.tanh(logits / CAP)
    vocab_rows = embed.shape[0]
    first_id = lax.axis_index(("fsdp", "mp", "sub")) * vocab_rows
    ids = first_id + jnp.arange(vocab_rows, dtype=jnp.int32)
    hits = all_targets[:, None] == ids[None, :]
    exp_sums, target_logits = lax.psum(
        (jnp.sum(jnp.exp(capped), axis=1), jnp.sum(jnp.where(hits, capped, 0.0), axis=1)),
        ("fsdp", "mp", "sub"),
    )
    own_start = lax.axis_index(("fsdp", "sub")) * tok_rows
    own_sums = lax.dynamic_slice_in_dim(exp_sums, own_start, tok_rows, 0)
    own_targets = lax.dynamic_slice_in_dim(target_logits, own_start, tok_rows, 0)
    weights = loss_mask.astype(jnp.float32)
    token_loss = weights * (jnp.log(own_sums) - own_targets)
    loss_sum, count = lax.psum((jnp.sum(token_loss), jnp.sum(weights)), ("fsdp", "sub"))
    mean_loss = (loss_sum / jnp.maximum(count, 1.0)).reshape(1)
    return (token_loss, mean_loss)


def solution(mesh):
    return jax.shard_map(
        on_device,
        mesh=mesh,
        in_specs=(
            P(("groups", "fsdp", "sub"), "mp"),
            P(("groups", "fsdp", "sub"), None),
            P("mp", "fsdp"),
            P("mp", "fsdp"),
            P(),
            P(),
            P(("fsdp", "mp", "sub"), None),
            P(("fsdp", "mp", "sub"), None),
            P(("groups", "fsdp", "sub")),
            P(("groups", "fsdp", "sub")),
        ),
        out_specs=(P(("groups", "fsdp", "sub")), P("groups")),
        check_vma=False,
    )
```

profile of v0, /device:TPU:0, one launch (start us, length us, event | category | flops | bytes accessed | tf_op | source)
XLA Modules:
  0.0 167.8 jit_solution(12297695420085963303)
XLA Ops:
  7.2 0.0 all-gather.2.cloned.1.call-start
  7.2 0.7 all-gather.2.cloned.1.call-update
  7.9 0.0 all-reduce.5.cloned.1.call-start
  8.0 0.1 shift_left.49
  8.1 17.8 %fusion.2 = bf16[18432,1152]{1,0:T(8,128)(2,1)} fusion(s32[18432]{0:T(1024)S(1)} %broadcast_bitcast_fusion, s32[2304,1152]{1,0:T(8,128)} %param.12, bf16[144,1152]{1,0:T(8,128)(2,1)} %param.13), kind=kLoop, calls=%fused_computation.3 | loop fusion | flops 148635648 | bytes 53489664 | tf_op jit(solution)/shard_map/mul | solution.py:19
  25.9 0.0 copy-start.7
  25.9 0.0 copy-start.6
  25.9 0.0 copy-start
  25.9 0.0 copy-start.3
  26.0 0.0 copy-start.1
  26.0 0.0 copy-start.2
  26.0 0.0 copy-start.4
  26.0 16.6 %all-gather.2.cloned.1.call-done = bf16[32,18432]{1,0:T(8,128)(2,1)} async-done(((bf16[8,18432]{1,0:T(8,128)(2,1)}), bf16[32,18432]{1,0:T(8,128)(2,1)}) %all-gather.2.cloned.1.call-update) | async-done | bytes 1179664 | tf_op jit(solution)/shard_map/all_gather | solution.py:54
  42.6 15.8 %convolution_bitcast_fusion = f32[4,8,1152]{2,1,0:T(8,128)S(1)} fusion(bf16[32,18432]{1,0:T(8,128)(2,1)} %all-gather.2.cloned.1.call-done, bf16[18432,1152]{1,0:T(8,128)(2,1)} %fusion.2), kind=kOutput, calls=%fused_computation.8 | convolution fusion | flops 1358954496 | bytes 43794432 | tf_op jit(solution)/shard_map/dot_general | solution.py:53
  58.4 0.0 copy-start.5
  58.4 9.7 %all_to_all.19 = f32[4,8,1152]{2,1,0:T(8,128)} all-to-all(f32[4,8,1152]{2,1,0:T(8,128)S(1)} %convolution_bitcast_fusion), channel_id=1, replica_groups=mesh['groups'=2,'fsdp'=4,'mp'=2,'sub'=2] {'fsdp'}, dimensions={0} | all-to-all | bytes 294912 | tf_op jit(solution)/shard_map/all_to_all | solution.py:58
  68.1 0.0 all-reduce.5.cloned.1.call-update
  68.1 0.1 shift_left.56
  68.2 0.1 shift_left.57
  68.3 0.0 copy-done.7
  68.3 0.6 dynamic-slice
  69.5 0.0 copy-done.6
  69.5 0.2 dynamic-update-slice
  69.8 0.0 copy-done
  69.8 0.0 copy-done.3
  69.8 3.6 %fusion.5 = bf16[512,4608]{0,1:T(8,128)(2,1)} fusion(s32[4608]{0:T(1024)S(1)} %shift_left.57, s32[512,576]{0,1:T(8,128)S(1)} %copy-done, bf16[512,36]{0,1:T(8,128)(2,1)S(1)} %copy-done.3), kind=kLoop, calls=%fused_computation.7 | loop fusion | flops 16515072 | bytes 5953536 | tf_op jit(solution)/shard_map/mul | solution.py:26
  73.4 6.5 %all-reduce = s32[64]{0:T(128)S(1)} all-reduce(s32[64]{0:T(128)S(1)} %dynamic-update-slice), channel_id=1, replica_groups=mesh['groups'=2,'fsdp'=4,'mp'=2,'sub'=2] {'fsdp','sub'}, use_global_device_ids=true, to_apply=%add | all-reduce | flops 64 | bytes 512
  79.8 8.8 %all-reduce.5.cloned.1.call-done = f32[8,4608]{1,0:T(8,128)} async-done(((f32[8,4608]{1,0:T(8,128)}), f32[8,4608]{1,0:T(8,128)}) %all-reduce.5.cloned.1.call-update) | async-done | bytes 147472 | tf_op jit(solution)/shard_map/psum | solution.py:31
  88.7 1.1 multiply_reduce_fusion.1
  89.7 0.0 copy-done.1
  89.8 0.0 copy-done.2
  89.8 1.1 multiply_reduce_fusion
  90.9 0.0 copy-done.4
  90.9 1.0 multiply_convert_fusion
  91.9 15.1 %all_gather.10 = bf16[64,4608]{1,0:T(8,128)(2,1)S(1)} all-gather(bf16[8,4608]{1,0:T(8,128)(2,1)S(1)} %multiply_convert_fusion), channel_id=1, replica_groups=mesh['groups'=2,'fsdp'=4,'mp'=2,'sub'=2] {'fsdp','sub'}, dimensions={0}, use_global_device_ids=true | all-gather | bytes 663552 | tf_op jit(solution)/shard_map/all_gather | solution.py:61
  107.0 3.4 %exponential_reduce_fusion = (f32[64]{0:T(128)S(1)}, f32[64]{0:T(128)S(1)}) fusion(s32[512]{0:T(512)S(1)} %iota_add_fusion, s32[64]{0:T(128)S(1)} %all-reduce, bf16[64,4608]{1,0:T(8,128)(2,1)S(1)} %all_gather.10, bf16[512,4608]{0,1:T(8,128)(2,1)} %fusion.5), kind=kOutput, calls=%fused_computation.17 | convolution fusion | flops 302186368 | bytes 5311232 | tf_op jit(solution)/shard_map/dot_general | solution.py:65
  110.4 32.7 %all-reduce.1 = (f32[64]{0:T(128)S(1)}, f32[64]{0:T(128)S(1)}) all-reduce(f32[64]{0:T(128)S(1)} %get-tuple-element.3, f32[64]{0:T(128)S(1)} %get-tuple-element.2), channel_id=1, replica_groups=mesh['groups'=2,'fsdp'=4,'mp'=2,'sub'=2] {'fsdp','mp','sub'}, use_global_device_ids=true, to_apply=%region_6.7 | all-reduce | flops 128 | bytes 1024 | tf_op jit(solution)/shard_map/psum | solution.py:73
  143.1 0.0 copy-done.5
  143.1 1.3 fusion.8
  144.4 14.2 %all-reduce.2 = (f32[]{:T(128)}, f32[]{:T(128)}) all-reduce(f32[]{:T(128)} %get-tuple-element.8, f32[]{:T(128)} %get-tuple-element.10), channel_id=1, replica_groups=mesh['groups'=2,'fsdp'=4,'mp'=2,'sub'=2] {'fsdp','sub'}, use_global_device_ids=true, to_apply=%region_8.9 | all-reduce | flops 2 | bytes 16 | tf_op jit(solution)/shard_map/psum | solution.py:82
  (7 shorter events, 0.0 us)
Async XLA Ops:
  7.2 35.4 %all-gather.2.cloned.1.call-start = ((), (), s32[]{:S(2)}) async-start(), calls=%async_computation.1 | async-start | bytes 1474560 | tf_op jit(solution)/shard_map/all_gather | solution.py:54
  7.9 80.8 %all-reduce.5.cloned.1.call-start = ((), (), s32[]{:S(2)}) async-start(), calls=%async_computation.2 | async-start | bytes 294912 | tf_op jit(solution)/shard_map/psum | solution.py:31
  25.9 42.4 %copy-start.7 = (u32[32]{0:T(128)S(1)}, u32[32]{0:T(128)}, u32[]{:S(2)}) copy-start(u32[32]{0:T(128)} %constant.48) | copy-start | bytes 388
  25.9 43.6 %copy-start.6 = (s32[8]{0:T(128)S(1)}, s32[8]{0:T(128)}, u32[]{:S(2)}) copy-start(s32[8]{0:T(128)} %param.18) | copy-start | bytes 100
  25.9 43.9 %copy-start = (s32[512,576]{0,1:T(8,128)S(1)}, s32[512,576]{0,1:T(8,128)}, u32[]{:S(2)}) copy-start(s32[512,576]{0,1:T(8,128)} %param.16) | copy-start | bytes 3538948
  25.9 43.8 %copy-start.3 = (bf16[512,36]{0,1:T(8,128)(2,1)S(1)}, bf16[512,36]{0,1:T(8,128)(2,1)}, u32[]{:S(2)}) copy-start(bf16[512,36]{0,1:T(8,128)(2,1)} %param.17) | copy-start | bytes 110596
  26.0 63.8 %copy-start.1 = (bf16[8,4608]{1,0:T(8,128)(2,1)S(1)}, bf16[8,4608]{1,0:T(8,128)(2,1)}, u32[]{:S(2)}) copy-start(bf16[8,4608]{1,0:T(8,128)(2,1)} %param.11) | copy-start | bytes 221188
  26.0 63.8 %copy-start.2 = (f32[4608]{0:T(1024)S(1)}, f32[4608]{0:T(1024)}, u32[]{:S(2)}) copy-start(f32[4608]{0:T(1024)} %param.14) | copy-start | bytes 55300
  26.0 64.9 %copy-start.4 = (f32[4608]{0:T(1024)S(1)}, f32[4608]{0:T(1024)}, u32[]{:S(2)}) copy-start(f32[4608]{0:T(1024)} %param.15) | copy-start | bytes 55300
  58.4 84.8 %copy-start.5 = (s32[8]{0:T(128)S(1)}, s32[8]{0:T(128)}, u32[]{:S(2)}) copy-start(s32[8]{0:T(128)} %param.19) | copy-start | bytes 100
Sparse Core Ops, SparseCore 0:
  9.5 32.9 all-gather.1
  68.2 20.3 all-reduce.4
where the time goes:
time: 168 us
  blocking collectives  78.2 us (47%)
  waiting for transfers between devices  26.1 us (16%)
  other arithmetic  25.9 us (15%)
  matrix products  19.2 us (11%)
  between operations  17.2 us (10%)
    psum x1, blocking collectives, on_device(): lax.psum((jnp.sum(jnp.exp(capped), axis=1), jnp.sum(jnp.where(hits, cappe...  32.7 us
    mul x1, other arithmetic, dequant_down(): grouped = codes.reshape(scales.shape[0], -1, cols) * scales[:, None, :]  17.8 us
    all_gather x1, waiting for transfers between devices, on_device(): lax.all_gather(hidden, 'fsdp', axis=0, tiled=True)  16.6 us
    dot_general x1, matrix products, on_device(): jnp.dot(lax.all_gather(hidden, 'fsdp', axis=0, tiled=True), local_weight,...  15.8 us
    all_gather x1, blocking collectives, on_device(): lax.all_gather(states, ('fsdp', 'sub'), axis=0, tiled=True)  15.1 us
    psum x1, blocking collectives, on_device(): lax.psum((jnp.sum(token_loss), jnp.sum(weights)), ('fsdp', 'sub'))  14.2 us
    all_to_all x1, blocking collectives, on_device(): lax.all_to_all(partial_cols, 'fsdp', split_axis=0, concat_axis=1, tiled=T...  9.71 us
    psum x1, waiting for transfers between devices, normalize_rows(): ffn = lax.psum(ffn, 'mp')  8.84 us
  transfers between devices with their start and end apart: 2, of which 2 were waited for; matrix products, arithmetic and copies ran while one was open for 13% of the time, Pallas kernels for 0%

commit v1 on v0

--- a/solution.py
+++ b/solution.py
@@ -28,7 +28,7 @@
 
 
 def normalize_rows(ffn, residual, post_gain, final_gain):
-    ffn = lax.psum(ffn, "mp")
+    ffn = jnp.sum(lax.all_gather(ffn, "mp"), axis=0)
     normed = ffn * lax.rsqrt(jnp.mean(ffn * ffn, axis=-1, keepdims=True) + EPS) * post_gain
     stream = residual.astype(jnp.float32) + normed
     return (

time: 168 us -> 159 us (0.946)
  waiting for transfers between devices: 26.1 us -> 17.3 us
  starting transfers between devices: 0.08 us -> 3.5 us
  other arithmetic: 25.9 us -> 23.2 us
  blocking collectives: 78.2 us -> 75.6 us
  matrix products: 19.2 us -> 21.1 us
    all_to_all x1 -> x0, blocking collectives: 9.71 us -> none  [on_device(): lax.all_to_all(partial_cols, 'fsdp', split_axis=0, concat_axis=1, tiled=T...]
    psum x1 -> x0, waiting for transfers between devices: 8.84 us -> none  [normalize_rows(): ffn = lax.psum(ffn, 'mp')]
    all_gather x0 -> x1, blocking collectives: none -> 5.81 us  [normalize_rows(): ffn = jnp.sum(lax.all_gather(ffn, 'mp'), axis=0)]
    all_to_all x0 -> x1, starting transfers between devices: none -> 3.47 us  [on_device(): lax.all_to_all(partial_cols, 'fsdp', split_axis=0, concat_axis=1, tiled=T...]
    unnamed x1, blocking collectives: 6.46 us -> 9.34 us
    dot_general x1, matrix products: 15.8 us -> 17.7 us  [on_device(): jnp.dot(lax.all_gather(hidden, 'fsdp', axis=0, tiled=True), local_weight,...]
  transfers between devices with their start and end apart: 2 -> 2, of which waited for: 2 -> 1; matrix products, arithmetic and copies ran while one was open for 13% -> 14% of each run, Pallas kernels for 0% -> 0%
where the time goes in v1:
time: 159 us
  blocking collectives  75.6 us (48%)
  other arithmetic  23.2 us (15%)
  matrix products  21.1 us (13%)
  waiting for transfers between devices  17.3 us (11%)
  between operations  17.2 us (11%)
  starting transfers between devices  3.5 us (2%)
    psum x1, blocking collectives, on_device(): lax.psum((jnp.sum(jnp.exp(capped), axis=1), jnp.sum(jnp.where(hits, cappe...  31.2 us
    mul x1, other arithmetic, dequant_down(): grouped = codes.reshape(scales.shape[0], -1, cols) * scales[:, None, :]  17.8 us
    dot_general x1, matrix products, on_device(): jnp.dot(lax.all_gather(hidden, 'fsdp', axis=0, tiled=True), local_weight,...  17.7 us
    all_gather x1, waiting for transfers between devices, on_device(): lax.all_gather(hidden, 'fsdp', axis=0, tiled=True)  16.6 us
    all_gather x1, blocking collectives, on_device(): lax.all_gather(states, ('fsdp', 'sub'), axis=0, tiled=True)  15 us
    psum x1, blocking collectives, on_device(): lax.psum((jnp.sum(token_loss), jnp.sum(weights)), ('fsdp', 'sub'))  14.2 us
    unnamed x1, blocking collectives  9.34 us
    all_gather x1, blocking collectives, normalize_rows(): ffn = jnp.sum(lax.all_gather(ffn, 'mp'), axis=0)  5.81 us
  transfers between devices with their start and end apart: 2, of which 1 were waited for; matrix products, arithmetic and copies ran while one was open for 14% of the time, Pallas kernels for 0%

profile of v1, /device:TPU:0, one launch (start us, length us, event | category | flops | bytes accessed | tf_op | source)
XLA Modules:
  0.0 159.0 jit_solution(1018941785445668045)
XLA Ops:
  7.2 0.0 all-gather.2.cloned.1.call-start
  7.2 0.7 all-gather.2.cloned.1.call-update
  7.9 0.1 shift_left.49
  8.0 17.8 %fusion.2 = bf16[18432,1152]{1,0:T(8,128)(2,1)} fusion(s32[18432]{0:T(1024)S(1)} %broadcast_bitcast_fusion, s32[2304,1152]{1,0:T(8,128)} %param.12, bf16[144,1152]{1,0:T(8,128)(2,1)} %param.13), kind=kLoop, calls=%fused_computation.3 | loop fusion | flops 148635648 | bytes 53489664 | tf_op jit(solution)/shard_map/mul | solution.py:19
  25.9 0.0 copy-start.7
  25.9 0.0 copy-start.6
  25.9 0.0 copy-start
  25.9 0.0 copy-start.3
  25.9 0.0 copy-start.1
  25.9 0.0 copy-start.2
  25.9 0.0 copy-start.4
  25.9 16.6 %all-gather.2.cloned.1.call-done = bf16[32,18432]{1,0:T(8,128)(2,1)} async-done(((bf16[8,18432]{1,0:T(8,128)(2,1)}), bf16[32,18432]{1,0:T(8,128)(2,1)}) %all-gather.2.cloned.1.call-update) | async-done | bytes 1179664 | tf_op jit(solution)/shard_map/all_gather | solution.py:54
  42.6 17.7 %convolution_bitcast_fusion = f32[4,8,1152]{2,1,0:T(8,128)} fusion(bf16[32,18432]{1,0:T(8,128)(2,1)} %all-gather.2.cloned.1.call-done, bf16[18432,1152]{1,0:T(8,128)(2,1)} %fusion.2), kind=kOutput, calls=%fused_computation.8 | convolution fusion | flops 1358954496 | bytes 43794432 | tf_op jit(solution)/shard_map/dot_general | solution.py:53
  60.3 0.0 copy-start.5
  60.3 3.5 %all-to-all-start = ((f32[4,8,1152]{2,1,0:T(8,128)}), f32[4,8,1152]{2,1,0:T(8,128)S(1)}, u32[]{:S(2)}, u32[]{:S(2)}) async-start(f32[4,8,1152]{2,1,0:T(8,128)} %convolution_bitcast_fusion), calls=%async_computation | async-start | bytes 294912 | tf_op jit(solution)/shard_map/all_to_all | solution.py:58
  63.8 0.1 shift_left.56
  63.8 0.1 shift_left.57
  63.9 0.0 copy-done.7
  63.9 0.6 dynamic-slice
  65.2 0.0 copy-done.6
  65.2 0.2 dynamic-update-slice
  65.4 0.0 copy-done
  65.4 0.0 copy-done.3
  65.4 3.6 %fusion.5 = bf16[512,4608]{0,1:T(8,128)(2,1)} fusion(s32[4608]{0:T(1024)S(1)} %shift_left.57, s32[512,576]{0,1:T(8,128)S(1)} %copy-done, bf16[512,36]{0,1:T(8,128)(2,1)S(1)} %copy-done.3), kind=kLoop, calls=%fused_computation.7 | loop fusion | flops 16515072 | bytes 5953536 | tf_op jit(solution)/shard_map/mul | solution.py:26
  69.0 9.3 %all-reduce = s32[64]{0:T(128)S(1)} all-reduce(s32[64]{0:T(128)S(1)} %dynamic-update-slice), channel_id=1, replica_groups=mesh['groups'=2,'fsdp'=4,'mp'=2,'sub'=2] {'fsdp','sub'}, use_global_device_ids=true, to_apply=%add | all-reduce | flops 64 | bytes 512
  78.3 0.0 all-to-all-done
  78.3 5.8 %all_gather.17 = f32[2,8,4608]{2,1,0:T(8,128)S(1)} all-gather(f32[1,8,4608]{2,1,0:T(8,128)S(1)} %bitcast.35), channel_id=1, replica_groups=mesh['groups'=2,'fsdp'=4,'mp'=2,'sub'=2] {'mp'}, dimensions={0}, use_global_device_ids=true | all-gather | bytes 442368 | tf_op jit(solution)/shard_map/all_gather | solution.py:31
  84.2 0.2 multiply_reduce_fusion.1
  84.3 0.0 copy-done.1
  84.3 0.0 copy-done.2
  84.3 0.2 multiply_reduce_fusion
  84.6 0.0 copy-done.4
  84.6 0.1 multiply_convert_fusion
  84.7 15.0 %all_gather.18 = bf16[64,4608]{1,0:T(8,128)(2,1)S(1)} all-gather(bf16[8,4608]{1,0:T(8,128)(2,1)S(1)} %multiply_convert_fusion), channel_id=1, replica_groups=mesh['groups'=2,'fsdp'=4,'mp'=2,'sub'=2] {'fsdp','sub'}, dimensions={0}, use_global_device_ids=true | all-gather | bytes 663552 | tf_op jit(solution)/shard_map/all_gather | solution.py:61
  99.7 3.4 %exponential_reduce_fusion = (f32[64]{0:T(128)S(1)}, f32[64]{0:T(128)S(1)}) fusion(s32[512]{0:T(512)S(1)} %iota_add_fusion, s32[64]{0:T(128)S(1)} %all-reduce, bf16[64,4608]{1,0:T(8,128)(2,1)S(1)} %all_gather.18, bf16[512,4608]{0,1:T(8,128)(2,1)} %fusion.5), kind=kOutput, calls=%fused_computation.17 | convolution fusion | flops 302186368 | bytes 5311232 | tf_op jit(solution)/shard_map/dot_general | solution.py:65
  103.1 31.2 %all-reduce.1 = (f32[64]{0:T(128)S(1)}, f32[64]{0:T(128)S(1)}) all-reduce(f32[64]{0:T(128)S(1)} %get-tuple-element.3, f32[64]{0:T(128)S(1)} %get-tuple-element.2), channel_id=1, replica_groups=mesh['groups'=2,'fsdp'=4,'mp'=2,'sub'=2] {'fsdp','mp','sub'}, use_global_device_ids=true, to_apply=%region_6.7 | all-reduce | flops 128 | bytes 1024 | tf_op jit(solution)/shard_map/psum | solution.py:73
  134.3 0.0 copy-done.5
  134.3 1.3 fusion.8
  135.6 14.2 %all-reduce.2 = (f32[]{:T(128)}, f32[]{:T(128)}) all-reduce(f32[]{:T(128)} %get-tuple-element.8, f32[]{:T(128)} %get-tuple-element.10), channel_id=1, replica_groups=mesh['groups'=2,'fsdp'=4,'mp'=2,'sub'=2] {'fsdp','sub'}, use_global_device_ids=true, to_apply=%region_8.9 | all-reduce | flops 2 | bytes 16 | tf_op jit(solution)/shard_map/psum | solution.py:82
  (8 shorter events, 0.1 us)
Async XLA Ops:
  7.2 35.4 %all-gather.2.cloned.1.call-start = ((), (), s32[]{:S(2)}) async-start(), calls=%async_computation.1 | async-start | bytes 1474560 | tf_op jit(solution)/shard_map/all_gather | solution.py:54
  25.9 38.0 %copy-start.7 = (u32[32]{0:T(128)S(1)}, u32[32]{0:T(128)}, u32[]{:S(2)}) copy-start(u32[32]{0:T(128)} %constant.48) | copy-start | bytes 388
  25.9 39.3 %copy-start.6 = (s32[8]{0:T(128)S(1)}, s32[8]{0:T(128)}, u32[]{:S(2)}) copy-start(s32[8]{0:T(128)} %param.18) | copy-start | bytes 100
  25.9 39.5 %copy-start = (s32[512,576]{0,1:T(8,128)S(1)}, s32[512,576]{0,1:T(8,128)}, u32[]{:S(2)}) copy-start(s32[512,576]{0,1:T(8,128)} %param.16) | copy-start | bytes 3538948
  25.9 39.5 %copy-start.3 = (bf16[512,36]{0,1:T(8,128)(2,1)S(1)}, bf16[512,36]{0,1:T(8,128)(2,1)}, u32[]{:S(2)}) copy-start(bf16[512,36]{0,1:T(8,128)(2,1)} %param.17) | copy-start | bytes 110596
  25.9 58.4 %copy-start.1 = (bf16[8,4608]{1,0:T(8,128)(2,1)S(1)}, bf16[8,4608]{1,0:T(8,128)(2,1)}, u32[]{:S(2)}) copy-start(bf16[8,4608]{1,0:T(8,128)(2,1)} %param.11) | copy-start | bytes 221188
  25.9 58.4 %copy-start.2 = (f32[4608]{0:T(1024)S(1)}, f32[4608]{0:T(1024)}, u32[]{:S(2)}) copy-start(f32[4608]{0:T(1024)} %param.14) | copy-start | bytes 55300
  25.9 58.6 %copy-start.4 = (f32[4608]{0:T(1024)S(1)}, f32[4608]{0:T(1024)}, u32[]{:S(2)}) copy-start(f32[4608]{0:T(1024)} %param.15) | copy-start | bytes 55300
  60.3 74.1 %copy-start.5 = (s32[8]{0:T(128)S(1)}, s32[8]{0:T(128)}, u32[]{:S(2)}) copy-start(s32[8]{0:T(128)} %param.19) | copy-start | bytes 100
  60.3 18.1 %all-to-all-start = ((f32[4,8,1152]{2,1,0:T(8,128)}), f32[4,8,1152]{2,1,0:T(8,128)S(1)}, u32[]{:S(2)}, u32[]{:S(2)}) async-start(f32[4,8,1152]{2,1,0:T(8,128)} %convolution_bitcast_fusion), calls=%async_computation | async-start | bytes 294912 | tf_op jit(solution)/shard_map/all_to_all | solution.py:58
Sparse Core Ops, SparseCore 0:
  9.5 32.9 all-gather.1
